TPU v7x, 256 devices: a whole 4x4x8 slice. The times are simulated.
256 devices in a mesh: ctx: 64 (over z, x_hi, y), tp: 4 (over x_lo, core).
Axes of the slice: x: 4 (x_hi: 2, x_lo: 2; x = x_hi * 2 + x_lo), y: 4, z: 8, core: 2. Of those that a mesh axis runs over, the one named last changes fastest.
Arguments:
- queries: bfloat16 [32768, 4096], P('ctx', 'tp'), may hold values from -22 to 22
- keys: bfloat16 [32768, 512], P('ctx', 'tp'), may hold values from -22 to 22
- values: bfloat16 [32768, 512], P('ctx', 'tp'), may hold values from -36 to 36
- positions: int32 [3, 32768], P(None, 'ctx'), may hold values from 0 to 32767
- segment_ids: int32 [32768], replicated, may hold values from 0 to 31, never falling along the last dimension, each value on 1 to 2048 neighbouring positions
- out_weight: bfloat16 [4096, 8192], P('tp', 'ctx'), may hold values from -0.09375 to 0.09375
- residual: bfloat16 [32768, 8192], P(('ctx', 'tp')), may hold values from -3 to 3
Outputs:
- layer_out: bfloat16 [32768, 8192], P(('ctx', 'tp'))
Inputs may be any that keep to these rules, and one draw needn't show every extreme that they name: `segment_ids`: ids never fall along the sequence; each document has 1 to 2048 tokens, and one has exactly 2048.
All inputs are finite; a program needn't handle non-finite values.
Results may differ from a plain program's by a relative error of at most 0.013.
Values may be sent and summed in bfloat16 or wider, within the bound.
A program may use at most 128 MiB of HBM per device.

v0:
```python
import math
import jax
import jax.numpy as jnp
from jax import lax
from jax.sharding import PartitionSpec as P

HD = 128
DOC = 2048
theta_base = 1000000.0


def from_behind(block, axis, distance):
    devices = range(lax.axis_size(axis))
    route = [(i - distance, i) for i in devices if i - distance in devices]
    return lax.ppermute(block, axis, route)


def rotary_tables(positions):
    half_dim = HD // 2
    freq_index = jnp.arange(half_dim)
    inv_freq = theta_base ** (-2.0 * freq_index.astype(jnp.float32) / HD)
    first_end = HD // 8
    second_end = first_end + 3 * HD // 16
    place = positions.astype(jnp.float32)
    chosen = jnp.where(
        freq_index[None, :] < first_end,
        place[0][:, None],
        jnp.where(freq_index[None, :] < second_end, place[1][:, None], place[2][:, None]),
    )
    angle = chosen * inv_freq[None, :]
    return (jnp.cos(angle), jnp.sin(angle))


def rotate(vectors, cosine_table, sine_table):
    half_dim = HD // 2
    lower_half = vectors[..., :half_dim]
    upper_half = vectors[..., half_dim:]
    cos_b = cosine_table[:, None, :]
    sin_b = sine_table[:, None, :]
    return jnp.concatenate(
        [lower_half * cos_b - upper_half * sin_b, upper_half * cos_b + lower_half * sin_b], axis=-1
    )


def on_device(queries, keys, values, positions, segment_ids, out_weight, residual):
    tok_rows = queries.shape[0]
    local_heads = queries.shape[1] // HD
    local_kv = keys.shape[1] // HD
    group_size = local_heads // local_kv
    reach_blocks = (DOC + tok_rows - 2) // tok_rows
    my_start = lax.axis_index("ctx") * tok_rows
    cosine_table, sine_table = rotary_tables(positions)
    rot_q = rotate(
        queries.reshape(tok_rows, local_heads, HD).astype(jnp.float32), cosine_table, sine_table
    ).astype(jnp.bfloat16)
    grouped = rot_q.reshape(tok_rows, local_kv, group_size, HD).transpose(1, 2, 0, 3)
    rot_k = rotate(
        keys.reshape(tok_rows, local_kv, HD).astype(jnp.float32), cosine_table, sine_table
    ).astype(jnp.bfloat16)
    key_flat = rot_k.reshape(tok_rows, local_kv * HD)
    query_index = my_start + jnp.arange(tok_rows, dtype=jnp.int32)
    query_seg = lax.dynamic_slice_in_dim(segment_ids, my_start, tok_rows, 0)
    score_scale = 1.0 / math.sqrt(HD)
    block_rows = math.gcd(tok_rows, 512)
    block_count = tok_rows // block_rows

    def absorb(running, stacked, offset):
        key_blocks = stacked[0].reshape(block_count, block_rows, local_kv, HD)
        value_blocks = stacked[1].reshape(block_count, block_rows, local_kv, HD)

        def advance(block_index, carried):
            key_block = lax.dynamic_index_in_dim(key_blocks, block_index, 0, keepdims=False)
            value_block = lax.dynamic_index_in_dim(value_blocks, block_index, 0, keepdims=False)
            key_first = offset + block_index * block_rows
            key_index = key_first + jnp.arange(block_rows, dtype=jnp.int32)
            key_seg = lax.dynamic_slice_in_dim(
                segment_ids, jnp.maximum(key_first, 0), block_rows, 0
            )
            allowed = (
                (key_index[None, :] <= query_index[:, None])
                & (key_index[None, :] >= 0)
                & (key_seg[None, :] == query_seg[:, None])
            )

            def update(current):
                row_peak, row_sum, weighted = current
                score = (
                    jnp.einsum(
                        "kgtd,nkd->kgtn", grouped, key_block, preferred_element_type=jnp.float32
                    )
                    * score_scale
                )
                score = jnp.where(allowed, score, -1e30)
                new_peak = jnp.maximum(row_peak, jnp.max(score, axis=-1))
                prob = jnp.where(allowed, jnp.exp(score - new_peak[..., None]), 0.0)
                rescale = jnp.exp(row_peak - new_peak)
                row_sum = row_sum * rescale + jnp.sum(prob, axis=-1)
                weighted = weighted * rescale[..., None] + jnp.einsum(
                    "kgtn,nkd->kgtd",
                    prob.astype(jnp.bfloat16),
                    value_block,
                    preferred_element_type=jnp.float32,
                )
                return (new_peak, row_sum, weighted)

            def keep_state(current):
                return current

            return lax.cond(jnp.any(allowed), update, keep_state, carried)

        return lax.fori_loop(0, block_count, advance, running)

    initial = (
        jnp.full((local_kv, group_size, tok_rows), -1e30, jnp.float32),
        jnp.zeros((local_kv, group_size, tok_rows), jnp.float32),
        jnp.zeros((local_kv, group_size, tok_rows, HD), jnp.float32),
    )
    own_pair = jnp.stack([key_flat, values], axis=0)
    state = absorb(initial, own_pair, my_start)

    def next_block(step_index, carried):
        moving, running = carried
        moving = from_behind(moving, "ctx", 1)
        running = absorb(running, moving, my_start - step_index * tok_rows)
        return (moving, running)

    moving, state = lax.fori_loop(1, reach_blocks + 1, next_block, (own_pair, state))
    row_peak, row_sum, weighted = state
    attended = (
        (weighted / row_sum[..., None])
        .transpose(2, 0, 1, 3)
        .reshape(tok_rows, local_heads * HD)
        .astype(jnp.bfloat16)
    )
    partial_sum = jnp.dot(
        attended,
        lax.all_gather(out_weight, "ctx", axis=1, tiled=True),
        preferred_element_type=jnp.float32,
    )
    partial_sum = partial_sum.astype(jnp.bfloat16).astype(jnp.float32)
    shared = lax.psum_scatter(
        partial_sum.astype(jnp.bfloat16), "tp", scatter_dimension=0, tiled=True
    ).astype(jnp.float32)
    return (shared + residual.astype(jnp.float32)).astype(jnp.bfloat16)


def solution(mesh):
    return jax.shard_map(
        on_device,
        mesh=mesh,
        in_specs=(
            P("ctx", "tp"),
            P("ctx", "tp"),
            P("ctx", "tp"),
            P(None, "ctx"),
            P(),
            P("tp", "ctx"),
            P(("ctx", "tp"), None),
        ),
        out_specs=P(("ctx", "tp"), None),
        check_vma=False,
    )
```

profile of v0, /device:TPU:1, one launch (start us, length us, event | category | flops | bytes accessed | tf_op | source)
XLA Modules:
  0.0 394.7 jit_solution(13520080402836505690)
XLA Ops:
  6.5 0.0 all-gather.2.cloned.1.call-start
  6.5 0.7 all-gather.2.cloned.1.call-update
  7.3 0.0 reduce-scatter.2.cloned.1.call-start
  7.3 0.7 convert_element_type.93
  8.0 1.5 copy.12
  9.5 0.3 convert.25
  9.8 0.8 fusion.44
  10.7 1.0 fusion.43
  12.3 0.0 copy-start.12
  12.4 0.0 copy-start.13
  12.4 0.0 copy-start.14
  12.4 0.0 copy-start.11
  12.4 0.0 copy-start.9
  12.4 0.0 copy-start.10
  12.4 0.6 fusion.41
  13.0 0.0 copy-done.7
  13.0 0.0 copy-done.12
  13.0 0.0 copy-done.13
  13.0 0.0 copy-done.14
  13.0 0.0 copy-done.11
  13.0 0.3 fusion.36
  13.4 0.1 maximum_bitcast_fusion
  13.5 0.7 copy.14
  14.1 0.0 copy-done.9
  14.2 0.0 copy-done.10
  14.2 1.5 broadcast_in_dim.135
  15.7 0.0 copy-done.5
  15.7 2.2 subtract_convert_fusion.1
  17.9 0.1 pad_maximum_fusion.1
  18.0 0.0 copy-start.8
  18.0 8.1 %conditional.2 = ((f32[1,8,512]{2,1,0:T(8,128)S(1)}, f32[1,8,512]{2,1,0:T(8,128)S(1)}, f32[1,8,512,128]{3,2,1,0:T(8,128)})) conditional(s32[]{:T(128)} %convert_element_type.95, (f32[1,8,512]{2,1,0:T(8,128)S(1)}, f32[1,8,512]{2,1,0:T(8,128)S(1)}, f32[1,8,512,128]{3,2,1,0:T(8,128)}) %tuple.39, (pred[512,512]{0,1:T(8,128)(4,1)S(1)}, ...), branch_computations={%region_1.2_spmd, %region_2.0_spmd} | conditional | flops 1102065664 | bytes 49021044 | solution.py:109
  18.0 0.0 copy-start
  18.0 0.0 copy-start.6
  18.0 1.5 fusion.2
  19.6 2.0 fusion.4
  21.6 0.0 copy-done
  21.6 3.1 bitcast_add_fusion
  24.8 0.0 copy-start.1
  24.8 1.3 copy-done.1
  26.1 1.0 pad_maximum_fusion
  27.1 47.2 %while.28 = (s32[]{:T(128)}, bf16[2,512,128]{2,1,0:T(8,128)(2,1)S(1)}, f32[1,8,512]{2,1,0:T(8,128)S(1)}, f32[1,8,512]{2,1,0:T(8,128)S(1)}, f32[1,8,512,128]{3,2,...) while((s32[]{:T(128)}, ...), condition=%wide.region_11.12_spmd.clone.clone, body=%wide.region_5.11_spmd.clone.clone.sunk | while | flops 1103378432 | bytes 50349432 | solution.py:127
  27.2 4.0 %collective-permute-start = (bf16[2,512,128]{2,1,0:T(8,128)(2,1)S(1)}, bf16[2,512,128]{2,1,0:T(8,128)(2,1)S(1)}, u32[]{:S(2)}, u32[]{:S(2)}) collective-permute-start(bf16[2,512,128]{2,1,0:T(8,128)(2,1)S(1)} %get-tuple-element.546), channel_id=1, source_target_pairs={{0,4},{4,8},{8,12},{12,16},{16,20},{20,24},{24,28},{28,32},{32,36}... | collective-permute-start | bytes 786440 | tf_op jit(solution)/shard_map/while/body/eval_jaxpr/ppermute | solution.py:15
  31.3 0.8 dynamic_slice.35
  32.0 1.1 fusion.49
  33.8 2.9 collective-permute-done
  36.7 11.1 %collective-permute-start = (bf16[2,512,128]{2,1,0:T(8,128)(2,1)S(1)}, bf16[2,512,128]{2,1,0:T(8,128)(2,1)S(1)}, u32[]{:S(2)}, u32[]{:S(2)}) collective-permute-start(bf16[2,512,128]{2,1,0:T(8,128)(2,1)S(1)} %get-tuple-element.546), channel_id=1, source_target_pairs={{0,4},{4,8},{8,12},{12,16},{16,20},{20,24},{24,28},{28,32},{32,36}... | collective-permute-start | bytes 786440 | tf_op jit(solution)/shard_map/while/body/eval_jaxpr/ppermute | solution.py:15
  47.8 0.8 dynamic_slice.35
  48.6 1.1 fusion.49
  50.4 0.7 collective-permute-done
  51.1 3.8 collective-permute-start
  55.0 0.8 dynamic_slice.35
  55.8 1.1 fusion.49
  57.5 0.7 collective-permute-done
  58.3 12.8 %collective-permute-start = (bf16[2,512,128]{2,1,0:T(8,128)(2,1)S(1)}, bf16[2,512,128]{2,1,0:T(8,128)(2,1)S(1)}, u32[]{:S(2)}, u32[]{:S(2)}) collective-permute-start(bf16[2,512,128]{2,1,0:T(8,128)(2,1)S(1)} %get-tuple-element.546), channel_id=1, source_target_pairs={{0,4},{4,8},{8,12},{12,16},{16,20},{20,24},{24,28},{28,32},{32,36}... | collective-permute-start | bytes 786440 | tf_op jit(solution)/shard_map/while/body/eval_jaxpr/ppermute | solution.py:15
  71.1 0.8 dynamic_slice.35
  71.9 1.1 fusion.49
  73.7 0.7 collective-permute-done
  74.4 1.9 copy.15
  76.3 0.3 divide_convert_fusion
  76.6 209.5 %all-gather.2.cloned.1.call-done = bf16[1024,8192]{1,0:T(8,128)(2,1)} async-done(((bf16[1024,128]{1,0:T(8,128)(2,1)}), bf16[1024,8192]{1,0:T(8,128)(2,1)}) %all-gather.2.cloned.1.call-update) | async-done | bytes 16777232 | tf_op jit(solution)/shard_map/all_gather | solution.py:137
  286.1 16.9 %convolution_convert_fusion = bf16[512,8192]{1,0:T(8,128)(2,1)} fusion(bf16[512,1024]{0,1:T(8,128)(2,1)S(1)} %bitcast.79, bf16[1024,8192]{1,0:T(8,128)(2,1)} %all-gather.2.cloned.1.call-done), kind=kOutput, calls=%fused_computation.45 | convolution fusion | flops 8594128896 | bytes 26214400 | tf_op jit(solution)/shard_map/dot_general | solution.py:135
  303.1 0.0 reduce-scatter.2.cloned.1.call-update
  303.1 81.3 %reduce-scatter.2.cloned.1.call-done = bf16[128,8192]{1,0:T(8,128)(2,1)} async-done(((bf16[512,8192]{1,0:T(8,128)(2,1)}), bf16[128,8192]{1,0:T(8,128)(2,1)}) %reduce-scatter.2.cloned.1.call-update) | async-done | bytes 2097168 | tf_op jit(solution)/shard_map/reduce_scatter | solution.py:141
  384.4 3.4 add_convert_fusion
  (36 shorter events, 0.2 us)
Async XLA Ops:
  6.5 9.1 %copy-start.5 = (bf16[512,128]{1,0:T(8,128)(2,1)S(1)}, bf16[512,128]{1,0:T(8,128)(2,1)}, u32[]{:S(2)}) copy-start(bf16[512,128]{1,0:T(8,128)(2,1)} %param.14) | copy-start | bytes 393220
  6.5 279.6 %all-gather.2.cloned.1.call-start = ((), (), s32[]{:S(2)}) async-start(), calls=%async_computation.1 | async-start | bytes 17039360 | tf_op jit(solution)/shard_map/all_gather | solution.py:137
  7.3 377.1 %reduce-scatter.2.cloned.1.call-start = ((), (), s32[]{:S(2)}) async-start(), calls=%async_computation.2 | async-start | bytes 10485760 | tf_op jit(solution)/shard_map/reduce_scatter | solution.py:141
  10.7 2.3 copy-start.7
  12.3 0.7 copy-start.12
  12.4 0.7 copy-start.13
  12.4 0.7 copy-start.14
  12.4 0.6 copy-start.11
  12.4 1.7 copy-start.9
  12.4 1.7 copy-start.10
  18.0 9.2 %copy-start.8 = (s32[512]{0:T(512)S(1)}, s32[512]{0:T(512)}, u32[]{:S(2)}) copy-start(s32[512]{0:T(512)} %copy-done.7) | copy-start | bytes 6148
  18.0 3.6 copy-start
  18.0 3.6 copy-start.6
  24.8 1.3 copy-start.1
  27.2 9.5 %collective-permute-start = (bf16[2,512,128]{2,1,0:T(8,128)(2,1)S(1)}, bf16[2,512,128]{2,1,0:T(8,128)(2,1)S(1)}, u32[]{:S(2)}, u32[]{:S(2)}) collective-permute-start(bf16[2,512,128]{2,1,0:T(8,128)(2,1)S(1)} %get-tuple-element.546), channel_id=1, source_target_pairs={{0,4},{4,8},{8,12},{12,16},{16,20},{20,24},{24,28},{28,32},{32,36}... | collective-permute-start | bytes 786440 | tf_op jit(solution)/shard_map/while/body/eval_jaxpr/ppermute | solution.py:15
  36.7 14.3 %collective-permute-start = (bf16[2,512,128]{2,1,0:T(8,128)(2,1)S(1)}, bf16[2,512,128]{2,1,0:T(8,128)(2,1)S(1)}, u32[]{:S(2)}, u32[]{:S(2)}) collective-permute-start(bf16[2,512,128]{2,1,0:T(8,128)(2,1)S(1)} %get-tuple-element.546), channel_id=1, source_target_pairs={{0,4},{4,8},{8,12},{12,16},{16,20},{20,24},{24,28},{28,32},{32,36}... | collective-permute-start | bytes 786440 | tf_op jit(solution)/shard_map/while/body/eval_jaxpr/ppermute | solution.py:15
  51.1 7.1 %collective-permute-start = (bf16[2,512,128]{2,1,0:T(8,128)(2,1)S(1)}, bf16[2,512,128]{2,1,0:T(8,128)(2,1)S(1)}, u32[]{:S(2)}, u32[]{:S(2)}) collective-permute-start(bf16[2,512,128]{2,1,0:T(8,128)(2,1)S(1)} %get-tuple-element.546), channel_id=1, source_target_pairs={{0,4},{4,8},{8,12},{12,16},{16,20},{20,24},{24,28},{28,32},{32,36}... | collective-permute-start | bytes 786440 | tf_op jit(solution)/shard_map/while/body/eval_jaxpr/ppermute | solution.py:15
  58.3 16.1 %collective-permute-start = (bf16[2,512,128]{2,1,0:T(8,128)(2,1)S(1)}, bf16[2,512,128]{2,1,0:T(8,128)(2,1)S(1)}, u32[]{:S(2)}, u32[]{:S(2)}) collective-permute-start(bf16[2,512,128]{2,1,0:T(8,128)(2,1)S(1)} %get-tuple-element.546), channel_id=1, source_target_pairs={{0,4},{4,8},{8,12},{12,16},{16,20},{20,24},{24,28},{28,32},{32,36}... | collective-permute-start | bytes 786440 | tf_op jit(solution)/shard_map/while/body/eval_jaxpr/ppermute | solution.py:15
  303.1 81.4 %copy-start.4 = (bf16[128,8192]{1,0:T(8,128)(2,1)S(1)}, bf16[128,8192]{1,0:T(8,128)(2,1)}, u32[]{:S(2)}) copy-start(bf16[128,8192]{1,0:T(8,128)(2,1)} %param.19) | copy-start | bytes 6291460
Sparse Core Ops, SparseCore 0:
  10.7 275.3 all-gather.1
  303.2 81.1 reduce-scatter.1
where the time goes:
time: 395 us
  waiting for transfers between devices  296 us (75%)
  starting transfers between devices  31.8 us (8%)
  matrix products  21.6 us (5%)
  other arithmetic  17.3 us (4%)
  between operations  14.3 us (4%)
  local copies, waits for them, and re-layouts  10.1 us (3%)
    all_gather x1, waiting for transfers between devices, on_device(): lax.all_gather(out_weight, 'ctx', axis=1, tiled=True)  209 us
    reduce_scatter x1, waiting for transfers between devices, on_device(): lax.psum_scatter(partial_sum.astype(jnp.bfloat16), 'tp', scatter_dimensio...  81.3 us
    ppermute x4, starting transfers between devices, from_behind(): return lax.ppermute(block, axis, route)  31.7 us
    dot_general x1, matrix products, on_device(): jnp.dot(attended, lax.all_gather(out_weight, 'ctx', axis=1, tiled=True),...  16.9 us
  transfers between devices with their start and end apart: 6, of which 6 were waited for; matrix products, arithmetic and copies ran while one was open for 7% of the time, Pallas kernels for 0%

commit v1 on v0

--- a/solution.py
+++ b/solution.py
@@ -7,6 +7,13 @@
 HD = 128
 DOC = 2048
 theta_base = 1000000.0
+
+
+def swapped_in(array, name, dim):
+    peers = lax.axis_size(name)
+    blocks = jnp.stack([array for _ in range(peers)])
+    blocks = lax.all_to_all(blocks, name, split_axis=0, concat_axis=0)
+    return jnp.concatenate(blocks, axis=dim)
 
 
 def from_behind(block, axis, distance):
@@ -133,9 +140,7 @@
         .astype(jnp.bfloat16)
     )
     partial_sum = jnp.dot(
-        attended,
-        lax.all_gather(out_weight, "ctx", axis=1, tiled=True),
-        preferred_element_type=jnp.float32,
+        attended, swapped_in(out_weight, "ctx", 1), preferred_element_type=jnp.float32
     )
     partial_sum = partial_sum.astype(jnp.bfloat16).astype(jnp.float32)
     shared = lax.psum_scatter(

time: 395 us -> 596 us (1.51)
  waiting for transfers between devices: 296 us -> 468 us
  starting transfers between devices: 31.8 us -> 45.8 us
  matrix products: 21.6 us -> 34.4 us
    all_to_all x0 -> x1, waiting for transfers between devices: none -> 253 us  [swapped_in(): blocks = lax.all_to_all(blocks, name, split_axis=0, concat_axis=0)]
    all_gather x1 -> x0, waiting for transfers between devices: 209 us -> none  [on_device(): lax.all_gather(out_weight, 'ctx', axis=1, tiled=True)]
    reduce_scatter x1, waiting for transfers between devices: 81.3 us -> 152 us  [on_device(): lax.psum_scatter(partial_sum.astype(jnp.bfloat16), 'tp', scatter_dimensio...]
    ppermute x4, waiting for transfers between devices: 4.86 us -> 63 us  [from_behind(): return lax.ppermute(block, axis, route)]
    all_to_all x0 -> x1, starting transfers between devices: none -> 15.5 us  [swapped_in(): blocks = lax.all_to_all(blocks, name, split_axis=0, concat_axis=0)]
    dot_general x1, matrix products: 16.9 us -> 29.8 us  [on_device(): jnp.dot(attended, swapped_in(out_weight, 'ctx', 1), preferred_element_typ...]
    another operation x0 -> x1, local copies, waits for them, and re-layouts: none -> 5.97 us  [swapped_in(): blocks = jnp.stack([array for _ in range(peers)])]
  transfers between devices with their start and end apart: 6 -> 6, of which waited for: 6 -> 6; matrix products, arithmetic and copies ran while one was open for 7% -> 4% of each run, Pallas kernels for 0% -> 0%
where the time goes in v1:
time: 596 us
  waiting for transfers between devices  468 us (79%)
  starting transfers between devices  45.8 us (8%)
  matrix products  34.4 us (6%)
  local copies, waits for them, and re-layouts  14.9 us (2%)
  other arithmetic  14.9 us (2%)
  between operations  14.3 us (2%)
    all_to_all x1, waiting for transfers between devices, swapped_in(): blocks = lax.all_to_all(blocks, name, split_axis=0, concat_axis=0)  253 us
    reduce_scatter x1, waiting for transfers between devices, on_device(): lax.psum_scatter(partial_sum.astype(jnp.bfloat16), 'tp', scatter_dimensio...  152 us
    ppermute x4, waiting for transfers between devices, from_behind(): return lax.ppermute(block, axis, route)  63 us
    ppermute x4, starting transfers between devices, from_behind(): return lax.ppermute(block, axis, route)  30.3 us
    dot_general x1, matrix products, on_device(): jnp.dot(attended, swapped_in(out_weight, 'ctx', 1), preferred_element_typ...  29.8 us
    all_to_all x1, starting transfers between devices, swapped_in(): blocks = lax.all_to_all(blocks, name, split_axis=0, concat_axis=0)  15.5 us
  transfers between devices with their start and end apart: 6, of which 6 were waited for; matrix products, arithmetic and copies ran while one was open for 4% of the time, Pallas kernels for 0%

profile of v1, /device:TPU:1, one launch (start us, length us, event | category | flops | bytes accessed | tf_op | source)
XLA Modules:
  0.0 595.8 jit_solution(15161622666981778575)
XLA Ops:
  6.5 1.1 copy.16
  7.6 6.0 %stack.8 = bf16[64,1024,128]{1,2,0:T(8,128)(2,1)} broadcast(bf16[1024,128]{0,1:T(8,128)(2,1)S(1)} %copy.16), dimensions={1,2} | broadcast | bytes 17039360 | tf_op jit(solution)/shard_map/stack | solution.py:14
  13.6 0.0 copy-start.8
  13.6 0.0 copy-start.5
  13.6 15.5 %all-to-all-start = ((bf16[64,1024,128]{1,2,0:T(8,128)(2,1)}), bf16[64,1024,128]{1,2,0:T(8,128)(2,1)}, u32[]{:S(2)}, u32[]{:S(2)}) async-start(bf16[64,1024,128]{1,2,0:T(8,128)(2,1)} %stack.8), calls=%async_computation | async-start | bytes 33554432 | tf_op jit(solution)/shard_map/all_to_all | solution.py:15
  29.1 0.0 copy-start.6
  29.1 0.0 reduce-scatter.2.cloned.1.call-start
  29.2 0.0 copy-done.8
  29.2 0.8 fusion.44
  30.1 1.0 fusion.43
  31.7 0.0 copy-done.5
  31.7 0.0 copy-start.7
  31.8 0.5 copy.12
  32.3 0.3 convert.25
  32.6 0.6 fusion.41
  33.2 0.4 fusion.36
  33.6 0.1 maximum_bitcast_fusion
  33.7 0.7 copy.14
  34.4 1.5 broadcast_in_dim.135
  35.8 0.0 copy-done.6
  35.9 1.4 subtract_convert_fusion.1
  37.3 0.1 pad_maximum_fusion.1
  37.4 0.0 copy-done.7
  37.4 7.0 %conditional.2 = ((f32[1,8,512]{2,1,0:T(8,128)S(1)}, f32[1,8,512]{2,1,0:T(8,128)S(1)}, f32[1,8,512,128]{3,2,1,0:T(8,128)})) conditional(s32[]{:T(128)} %convert_element_type.95, (f32[1,8,512]{2,1,0:T(8,128)S(1)}, f32[1,8,512]{2,1,0:T(8,128)S(1)}, f32[1,8,512,128]{3,2,1,0:T(8,128)}) %tuple.39, (pred[512,512]{0,1:T(8,128)(4,1)S(1)}, ...), branch_computations={%region_1.2_spmd, %region_2.0_spmd} | conditional | flops 1102065664 | bytes 48496728 | solution.py:116
  37.4 0.0 copy-start
  37.4 1.5 fusion.2
  39.0 0.0 copy-done
  39.0 3.1 bitcast_add_fusion
  42.1 0.0 copy-start.1
  42.1 2.0 fusion.4
  44.2 0.0 copy-done.1
  44.4 0.1 pad_maximum_fusion
  44.5 103.7 %while.28 = (s32[]{:T(128)}, bf16[2,512,128]{2,1,0:T(8,128)(2,1)S(1)}, f32[1,8,512]{2,1,0:T(8,128)S(1)}, f32[1,8,512]{2,1,0:T(8,128)S(1)}, f32[1,8,512,128]{3,2,...) while((s32[]{:T(128)}, ...), condition=%wide.region_11.12_spmd.clone.clone, body=%wide.region_5.11_spmd.clone.clone.sunk | while | flops 1103378432 | bytes 50349432 | solution.py:134
  44.5 2.9 collective-permute-start
  47.5 0.8 dynamic_slice.35
  48.2 1.1 fusion.49
  50.0 49.7 %collective-permute-done = bf16[2,512,128]{2,1,0:T(8,128)(2,1)S(1)} collective-permute-done((bf16[2,512,128]{2,1,0:T(8,128)(2,1)S(1)}, bf16[2,512,128]{2,1,0:T(8,128)(2,1)S(1)}, u32[]{:S(2)}, u32[]{:S(2)}) %collective-permute-start) | collective-permute-done | bytes 262176 | tf_op jit(solution)/shard_map/while/body/eval_jaxpr/ppermute | solution.py:22
  99.7 12.6 %collective-permute-start = (bf16[2,512,128]{2,1,0:T(8,128)(2,1)S(1)}, bf16[2,512,128]{2,1,0:T(8,128)(2,1)S(1)}, u32[]{:S(2)}, u32[]{:S(2)}) collective-permute-start(bf16[2,512,128]{2,1,0:T(8,128)(2,1)S(1)} %get-tuple-element.546), channel_id=1, source_target_pairs={{0,4},{4,8},{8,12},{12,16},{16,20},{20,24},{24,28},{28,32},{32,36}... | collective-permute-start | bytes 786440 | tf_op jit(solution)/shard_map/while/body/eval_jaxpr/ppermute | solution.py:22
  112.4 0.8 dynamic_slice.35
  113.1 1.1 fusion.49
  114.9 10.4 %collective-permute-done = bf16[2,512,128]{2,1,0:T(8,128)(2,1)S(1)} collective-permute-done((bf16[2,512,128]{2,1,0:T(8,128)(2,1)S(1)}, bf16[2,512,128]{2,1,0:T(8,128)(2,1)S(1)}, u32[]{:S(2)}, u32[]{:S(2)}) %collective-permute-start) | collective-permute-done | bytes 262176 | tf_op jit(solution)/shard_map/while/body/eval_jaxpr/ppermute | solution.py:22
  125.3 4.4 collective-permute-start
  129.7 0.8 dynamic_slice.35
  130.5 1.1 fusion.49
  132.2 2.2 collective-permute-done
  134.5 10.4 %collective-permute-start = (bf16[2,512,128]{2,1,0:T(8,128)(2,1)S(1)}, bf16[2,512,128]{2,1,0:T(8,128)(2,1)S(1)}, u32[]{:S(2)}, u32[]{:S(2)}) collective-permute-start(bf16[2,512,128]{2,1,0:T(8,128)(2,1)S(1)} %get-tuple-element.546), channel_id=1, source_target_pairs={{0,4},{4,8},{8,12},{12,16},{16,20},{20,24},{24,28},{28,32},{32,36}... | collective-permute-start | bytes 786440 | tf_op jit(solution)/shard_map/while/body/eval_jaxpr/ppermute | solution.py:22
  145.0 0.8 dynamic_slice.35
  145.8 1.1 fusion.49
  147.5 0.7 collective-permute-done
  148.3 1.9 copy.15
  150.2 0.3 divide_convert_fusion
  150.5 252.9 %all-to-all-done = bf16[64,1024,128]{1,2,0:T(8,128)(2,1)} async-done(((bf16[64,1024,128]{1,2,0:T(8,128)(2,1)}), bf16[64,1024,128]{1,2,0:T(8,128)(2,1)}, u32[]{:S(2)}, u32[]{:S(2)}) %all-to-all-start) | async-done | bytes 16777248 | tf_op jit(solution)/shard_map/all_to_all | solution.py:15
  403.4 29.8 %convolution_convert_fusion = bf16[512,8192]{1,0:T(8,128)(2,1)} fusion(bf16[512,1024]{0,1:T(8,128)(2,1)S(1)} %bitcast.82, bf16[1024,8192]{0,1:T(8,128)(2,1)} %bitcast.36), kind=kOutput, calls=%fused_computation.45 | convolution fusion | flops 8594128896 | bytes 26214400 | tf_op jit(solution)/shard_map/dot_general | solution.py:142
  433.2 0.0 copy-start.4
  433.2 0.0 reduce-scatter.2.cloned.1.call-update
  433.3 152.3 %reduce-scatter.2.cloned.1.call-done = bf16[128,8192]{1,0:T(8,128)(2,1)} async-done(((bf16[512,8192]{1,0:T(8,128)(2,1)}), bf16[128,8192]{1,0:T(8,128)(2,1)}) %reduce-scatter.2.cloned.1.call-update) | async-done | bytes 2097168 | tf_op jit(solution)/shard_map/reduce_scatter | solution.py:146
  585.6 0.0 copy-done.4
  585.6 3.4 add_convert_fusion
  (31 shorter events, 0.2 us)
Async XLA Ops:
  13.6 15.6 %copy-start.8 = (s32[3,512]{1,0:T(4,128)S(1)}, s32[3,512]{1,0:T(4,128)}, u32[]{:S(2)}) copy-start(s32[3,512]{1,0:T(4,128)} %param.16) | copy-start | bytes 18436
  13.6 18.1 %copy-start.5 = (bf16[512,1024]{1,0:T(8,128)(2,1)S(1)}, bf16[512,1024]{1,0:T(8,128)(2,1)}, u32[]{:S(2)}) copy-start(bf16[512,1024]{1,0:T(8,128)(2,1)} %param.13) | copy-start | bytes 3145732
  13.6 389.8 %all-to-all-start = ((bf16[64,1024,128]{1,2,0:T(8,128)(2,1)}), bf16[64,1024,128]{1,2,0:T(8,128)(2,1)}, u32[]{:S(2)}, u32[]{:S(2)}) async-start(bf16[64,1024,128]{1,2,0:T(8,128)(2,1)} %stack.8), calls=%async_computation | async-start | bytes 33554432 | tf_op jit(solution)/shard_map/all_to_all | solution.py:15
  29.1 6.7 %copy-start.6 = (bf16[512,128]{1,0:T(8,128)(2,1)S(1)}, bf16[512,128]{1,0:T(8,128)(2,1)}, u32[]{:S(2)}) copy-start(bf16[512,128]{1,0:T(8,128)(2,1)} %param.14) | copy-start | bytes 393220
  29.1 556.5 %reduce-scatter.2.cloned.1.call-start = ((), (), s32[]{:S(2)}) async-start(), calls=%async_computation.2 | async-start | bytes 10485760 | tf_op jit(solution)/shard_map/reduce_scatter | solution.py:146
  31.7 5.6 copy-start.7
  37.4 1.6 copy-start
  42.1 2.1 copy-start.1
  44.5 55.1 %collective-permute-start = (bf16[2,512,128]{2,1,0:T(8,128)(2,1)S(1)}, bf16[2,512,128]{2,1,0:T(8,128)(2,1)S(1)}, u32[]{:S(2)}, u32[]{:S(2)}) collective-permute-start(bf16[2,512,128]{2,1,0:T(8,128)(2,1)S(1)} %get-tuple-element.546), channel_id=1, source_target_pairs={{0,4},{4,8},{8,12},{12,16},{16,20},{20,24},{24,28},{28,32},{32,36}... | collective-permute-start | bytes 786440 | tf_op jit(solution)/shard_map/while/body/eval_jaxpr/ppermute | solution.py:22
  99.7 25.5 %collective-permute-start = (bf16[2,512,128]{2,1,0:T(8,128)(2,1)S(1)}, bf16[2,512,128]{2,1,0:T(8,128)(2,1)S(1)}, u32[]{:S(2)}, u32[]{:S(2)}) collective-permute-start(bf16[2,512,128]{2,1,0:T(8,128)(2,1)S(1)} %get-tuple-element.546), channel_id=1, source_target_pairs={{0,4},{4,8},{8,12},{12,16},{16,20},{20,24},{24,28},{28,32},{32,36}... | collective-permute-start | bytes 786440 | tf_op jit(solution)/shard_map/while/body/eval_jaxpr/ppermute | solution.py:22
  125.3 9.2 %collective-permute-start = (bf16[2,512,128]{2,1,0:T(8,128)(2,1)S(1)}, bf16[2,512,128]{2,1,0:T(8,128)(2,1)S(1)}, u32[]{:S(2)}, u32[]{:S(2)}) collective-permute-start(bf16[2,512,128]{2,1,0:T(8,128)(2,1)S(1)} %get-tuple-element.546), channel_id=1, source_target_pairs={{0,4},{4,8},{8,12},{12,16},{16,20},{20,24},{24,28},{28,32},{32,36}... | collective-permute-start | bytes 786440 | tf_op jit(solution)/shard_map/while/body/eval_jaxpr/ppermute | solution.py:22
  134.5 13.7 %collective-permute-start = (bf16[2,512,128]{2,1,0:T(8,128)(2,1)S(1)}, bf16[2,512,128]{2,1,0:T(8,128)(2,1)S(1)}, u32[]{:S(2)}, u32[]{:S(2)}) collective-permute-start(bf16[2,512,128]{2,1,0:T(8,128)(2,1)S(1)} %get-tuple-element.546), channel_id=1, source_target_pairs={{0,4},{4,8},{8,12},{12,16},{16,20},{20,24},{24,28},{28,32},{32,36}... | collective-permute-start | bytes 786440 | tf_op jit(solution)/shard_map/while/body/eval_jaxpr/ppermute | solution.py:22
  433.2 152.4 %copy-start.4 = (bf16[128,8192]{1,0:T(8,128)(2,1)S(1)}, bf16[128,8192]{1,0:T(8,128)(2,1)}, u32[]{:S(2)}) copy-start(bf16[128,8192]{1,0:T(8,128)(2,1)} %param.19) | copy-start | bytes 6291460
Sparse Core Ops, SparseCore 0:
  433.4 152.1 reduce-scatter.1
